TPU v7x, 32 devices: a whole 2x2x4 slice. The times are simulated.
32 devices in a mesh: dp: 8 (over y, x, core), expert: 4 (over z).
Axes of the slice: x: 2, y: 2, z: 4, core: 2. Of those that a mesh axis runs over, the one named last changes fastest.
Arguments:
- hidden_act: bfloat16 [4096, 2048], P('dp', 'expert'), may hold values from -6 to 6
- out_grad: bfloat16 [4096, 7168], P('dp'), may hold values from -0.125 to 0.125
- counts: int32 [8], P('dp'), may hold values from 0 to 512
- expert_master: float32 [7168, 2048], P('dp', 'expert'), may hold values from -0.005 to 0.005
- expert_mom: float32 [7168, 2048], P('dp', 'expert'), may hold values from -0.12 to 0.12
- expert_var: float32 [7168, 2048], P('dp', 'expert'), may hold values from 0.001 to 0.1
- dense_partial: float32 [8, 4, 14336], P('dp', 'expert'), may hold values from -0.8 to 0.8
- dense_master: float32 [14336], replicated, may hold values from 0.5 to 1.5
- dense_mom: float32 [14336], replicated, may hold values from -2 to 2
- dense_var: float32 [14336], replicated, may hold values from 0.1 to 10
Outputs:
- routed_weight: bfloat16 [7168, 2048], P(None, 'expert')
- new_expert_master: float32 [7168, 2048], P('dp', 'expert')
- new_expert_mom: float32 [7168, 2048], P('dp', 'expert')
- new_expert_var: float32 [7168, 2048], P('dp', 'expert')
- new_dense_master: float32 [14336], replicated
- new_dense_mom: float32 [14336], replicated
- new_dense_var: float32 [14336], replicated
All inputs are finite; a program needn't handle non-finite values.
Results may differ from a plain program's by a relative error of at most 0.0004.
Values may be sent and summed in bfloat16 or wider, within the bound.
A program may use at most 128 MiB of HBM per device.

v0:
```python
import jax
import jax.numpy as jnp
from jax import lax
from jax.sharding import PartitionSpec as P

beta_one = 0.9
beta_two = 0.95
learn_rate = 0.00022
decay_rate = 0.1
epsilon = 1e-08
step_count = 100


def adamw(gradient, master, moment, second):
    moment_new = beta_one * moment + (1.0 - beta_one) * gradient
    second_new = beta_two * second + (1.0 - beta_two) * gradient * gradient
    first_fix = 1.0 - beta_one**step_count
    second_fix = 1.0 - beta_two**step_count
    update = (
        moment_new / first_fix / (jnp.sqrt(second_new / second_fix) + epsilon) + decay_rate * master
    )
    return (master - learn_rate * update, moment_new, second_new)


def on_device(
    hidden_act,
    out_grad,
    counts,
    expert_master,
    expert_mom,
    expert_var,
    dense_partial,
    dense_master,
    dense_mom,
    dense_var,
):
    slots = hidden_act.shape[0]
    row_live = lax.iota(jnp.int32, slots) < counts[0]
    masked = jnp.where(row_live[:, None], hidden_act, jnp.zeros_like(hidden_act))
    dense_local = dense_partial.reshape(-1)
    expert_grad = lax.psum_scatter(
        lax.dot_general(
            out_grad, masked, (((0,), (0,)), ((), ())), preferred_element_type=jnp.float32
        ),
        "dp",
        scatter_dimension=0,
        tiled=True,
    )
    dense_grad = lax.psum(dense_local, ("dp", "expert"))
    dense_new, dense_moment, dense_second = adamw(dense_grad, dense_master, dense_mom, dense_var)
    master_new, moment_new, second_new = adamw(expert_grad, expert_master, expert_mom, expert_var)
    routed_weight = lax.all_gather(master_new.astype(jnp.bfloat16), "dp", axis=0, tiled=True)
    return (
        routed_weight,
        master_new,
        moment_new,
        second_new,
        dense_new,
        dense_moment,
        dense_second,
    )


def solution(mesh):
    in_specs = (
        P("dp", "expert"),
        P("dp", None),
        P("dp"),
        P("dp", "expert"),
        P("dp", "expert"),
        P("dp", "expert"),
        P("dp", "expert", None),
        P(),
        P(),
        P(),
    )
    out_specs = (
        P(None, "expert"),
        P("dp", "expert"),
        P("dp", "expert"),
        P("dp", "expert"),
        P(),
        P(),
        P(),
    )
    return jax.shard_map(
        on_device, mesh=mesh, in_specs=in_specs, out_specs=out_specs, check_vma=False
    )
```

profile of v0, /device:TPU:0, one launch (start us, length us, event | category | flops | bytes accessed | tf_op | source)
XLA Modules:
  0.0 200.4 jit_solution(5589663375833429149)
XLA Ops:
  7.2 0.0 reduce-scatter.2.cloned.1.call-start
  7.9 12.6 %convolution_bitcast_fusion = f32[7168,512]{0,1:T(8,128)} fusion(bf16[512,7168]{1,0:T(8,128)(2,1)} %param.11, bf16[512,512]{1,0:T(8,128)(2,1)} %param.10, pred[512]{0:T(512)(128)(4,1)S(1)} %iota_compare_fusion), kind=kOutput, calls=%fused_computation | convolution fusion | flops 3758358528 | bytes 22544896 | tf_op jit(solution)/shard_map/dot_general | solution.py:42
  20.5 0.0 copy-start
  20.5 0.0 reduce-scatter.2.cloned.1.call-update
  20.5 0.0 all-gather.2.cloned.1.call-start
  20.5 1.4 copy-done
  22.0 1.7 copy.17
  23.6 2.9 %copy.18 = f32[896,512]{0,1:T(8,128)} copy(f32[896,512]{1,0:T(8,128)} %param.15) | data formatting | bytes 3670016 | tf_op args[5]
  26.5 0.0 copy-done.1
  26.5 1.7 copy.20
  28.2 97.5 %reduce-scatter.2.cloned.1.call-done = f32[896,512]{0,1:T(8,128)} async-done(((f32[7168,512]{0,1:T(8,128)}), f32[896,512]{0,1:T(8,128)}) %reduce-scatter.2.cloned.1.call-update) | async-done | bytes 1835024 | tf_op jit(solution)/shard_map/reduce_scatter | solution.py:41
  125.6 6.9 %fusion.7 = (bf16[896,512]{0,1:T(8,128)(2,1)}, f32[896,512]{0,1:T(8,128)}, f32[896,512]{0,1:T(8,128)}, f32[896,512]{0,1:T(8,128)S(1)}) fusion(f32[896,512]{0,1:T(8,128)} %copy.20, f32[896,512]{0,1:T(8,128)} %reduce-scatter.2.cloned.1.call-done, f32[896,512]{0,1:T(8,128)} %copy.17, f32[896,512]{0,1:T(8,128)} %copy.18), kind=kLoop, calls=%fused_computation.14 | loop fusion | flops 7340032 | bytes 13762560 | tf_op jit(solution)/shard_map/convert_element_type | solution.py:52
  132.5 0.0 all-gather.2.cloned.1.call-update
  132.5 0.0 copy-done.5
  132.6 40.8 %psum.7 = f32[14336]{0:T(1024)S(1)} all-reduce(f32[14336]{0:T(1024)S(1)} %bitcast.6), channel_id=1, replica_groups=mesh['dp'=8,'expert'=4] {'dp','expert'}, use_global_device_ids=true, to_apply=%region_1.2 | all-reduce | flops 14336 | bytes 114688 | tf_op jit(solution)/shard_map/psum | solution.py:49
  173.3 0.0 copy-done.2
  173.3 0.0 copy-done.3
  173.3 0.0 copy-done.4
  173.3 0.7 multiply_subtract_fusion.1
  174.0 2.7 %copy.22 = f32[896,512]{1,0:T(8,128)} copy(f32[896,512]{0,1:T(8,128)} %get-tuple-element.18) | data formatting | bytes 3670016
  176.8 2.7 %copy.23 = f32[896,512]{1,0:T(8,128)} copy(f32[896,512]{0,1:T(8,128)} %get-tuple-element.19) | data formatting | bytes 3670016
  179.5 1.7 copy.24
  181.1 2.0 all-gather.2.cloned.1.call-done
  183.1 10.4 %copy.21 = bf16[7168,512]{1,0:T(8,128)(2,1)} copy(bf16[7168,512]{0,1:T(8,128)(2,1)} %all-gather.2.cloned.1.call-done) | data formatting | bytes 14680064
  (6 shorter events, 0.0 us)
Async XLA Ops:
  7.2 118.5 %reduce-scatter.2.cloned.1.call-start = ((), (), s32[]{:S(2)}) async-start(), calls=%async_computation.1 | async-start | bytes 16515072 | tf_op jit(solution)/shard_map/reduce_scatter | solution.py:41
  20.5 1.5 copy-start
  20.5 162.6 %all-gather.2.cloned.1.call-start = ((), (), s32[]{:S(2)}) async-start(), calls=%async_computation.2 | async-start | bytes 8257536 | tf_op jit(solution)/shard_map/all_gather | solution.py:52
  23.6 2.9 %copy-start.1 = (f32[896,512]{1,0:T(8,128)S(1)}, f32[896,512]{1,0:T(8,128)}, u32[]{:S(2)}) copy-start(f32[896,512]{1,0:T(8,128)} %param.13) | copy-start | bytes 5505028
  28.2 104.4 %copy-start.5 = (f32[1,1,14336]{2,1,0:T(1,128)S(1)}, f32[1,1,14336]{2,1,0:T(1,128)}, u32[]{:S(2)}) copy-start(f32[1,1,14336]{2,1,0:T(1,128)} %param.16) | copy-start | bytes 172036
  28.2 145.2 %copy-start.2 = (f32[14336]{0:T(1024)S(1)}, f32[14336]{0:T(1024)}, u32[]{:S(2)}) copy-start(f32[14336]{0:T(1024)} %param.17) | copy-start | bytes 172036
  28.2 145.2 %copy-start.3 = (f32[14336]{0:T(1024)S(1)}, f32[14336]{0:T(1024)}, u32[]{:S(2)}) copy-start(f32[14336]{0:T(1024)} %param.18) | copy-start | bytes 172036
  28.2 145.2 %copy-start.4 = (f32[14336]{0:T(1024)S(1)}, f32[14336]{0:T(1024)}, u32[]{:S(2)}) copy-start(f32[14336]{0:T(1024)} %param.19) | copy-start | bytes 172036
Sparse Core Ops, SparseCore 0:
  20.6 104.9 reduce-scatter.1
  132.7 50.4 all-gather.1
where the time goes:
time: 201 us; the launch traced here: 200 us
  waiting for transfers between devices  99.5 us (50%)
  blocking collectives  40.8 us (20%)
  local copies, waits for them, and re-layouts  25.2 us (13%)
  between operations  14.7 us (7%)
  matrix products  12.6 us (6%)
  other arithmetic  7.57 us (4%)
    reduce_scatter x1, waiting for transfers between devices, on_device(): lax.psum_scatter(lax.dot_general(out_grad, masked, (((0,), (0,)), ((), ()...  97.5 us
    psum x1, blocking collectives, on_device(): dense_grad = lax.psum(dense_local, ('dp', 'expert'))  40.8 us
    unnamed x19, local copies, waits for them, and re-layouts  25.2 us
    dot_general x1, matrix products, on_device(): lax.dot_general(out_grad, masked, (((0,), (0,)), ((), ())), preferred_ele...  12.6 us
    convert_element_type x1, other arithmetic, on_device(): master_new.astype(jnp.bfloat16)  6.88 us
  transfers between devices with their start and end apart: 2, of which 2 were waited for; matrix products, arithmetic and copies ran while one was open for 7% of the time, Pallas kernels for 0%

commit v1 on v0

--- a/solution.py
+++ b/solution.py
@@ -1,6 +1,10 @@
+import functools
+
 import jax
 import jax.numpy as jnp
 from jax import lax
+from jax.experimental import pallas as pl
+from jax.experimental.pallas import tpu as pltpu
 from jax.sharding import PartitionSpec as P
 
 beta_one = 0.9
@@ -61,6 +65,401 @@
     )
 
 
+MESH = pl.DeviceIdType.MESH
+LANES = 128
+DIAG, XN, YN, OWN = 0, 1, 2, 3
+TOP = 32767.0
+
+
+def adamw_kernel(gradient, master, moment, second):
+    moment_new = beta_one * moment + (1.0 - beta_one) * gradient
+    second_new = beta_two * second + (1.0 - beta_two) * gradient * gradient
+    first_fix = 1.0 / (1.0 - beta_one**step_count)
+    second_fix = 1.0 / (1.0 - beta_two**step_count)
+    update = (
+        moment_new * first_fix / (jnp.sqrt(second_new * second_fix) + epsilon) + decay_rate * master
+    )
+    return (master - learn_rate * update, moment_new, second_new)
+
+
+def fused_kernel(
+    n_z,
+    counts_ref,
+    hid_ref,
+    og_ref,
+    p_ref,
+    m_ref,
+    v_ref,
+    dpart_ref,
+    dp_ref,
+    dm_ref,
+    dv_ref,
+    w_out,
+    p_out,
+    m_out,
+    v_out,
+    dp_out,
+    dm_out,
+    dv_out,
+    hid_raw,
+    hid_own,
+    hid_peer,
+    og_own,
+    og_peer,
+    part,
+    q_send,
+    q_recv,
+    p_s,
+    m_s,
+    v_s,
+    w_all,
+    d_one,
+    d_two,
+    d_three,
+    d_four,
+    d_z,
+    d_tot,
+    load_sem,
+    store_sem,
+    in_send,
+    in_recv,
+    rs_send,
+    rs_recv,
+    ag_send,
+    ag_recv,
+    peer_send,
+    peer_recv,
+    place_sem,
+    d_send,
+    d_recv,
+):
+    me = lax.axis_index("dp")
+    z = lax.axis_index("expert")
+    core = lax.rem(me, 2)
+    x_at = lax.rem(lax.div(me, 2), 2)
+    y_at = lax.div(me, 4)
+    flip = 1 - 2 * core
+    peer = me + flip
+    x_next = me + 2 - 4 * x_at
+    y_next = me + 4 - 8 * y_at
+    diag = x_next + 4 - 8 * y_at
+    owners = (diag, x_next, y_next, me)
+    block = p_ref.shape[0]
+    width = p_ref.shape[1]
+    chunks = width // LANES
+    half = d_one.shape[0]
+
+    def og_cols(device):
+        return og_ref.at[:, pl.ds(pl.multiple_of(device * block, LANES), block)]
+
+    def cols(k):
+        return pl.ds(k * LANES, LANES)
+
+    loads = [pltpu.make_async_copy(hid_ref, hid_raw, load_sem.at[0])]
+    for s in range(4):
+        loads.append(pltpu.make_async_copy(og_cols(owners[s]), og_own.at[s], load_sem.at[1 + s]))
+    for i, (a, b) in enumerate(((p_ref, p_s), (m_ref, m_s), (v_ref, v_s))):
+        loads.append(pltpu.make_async_copy(a, b, load_sem.at[5 + i]))
+    for copy in loads:
+        copy.start()
+
+    barrier = pltpu.get_barrier_semaphore()
+    for device in (peer, x_next, y_next):
+        pl.semaphore_signal(barrier, inc=1, device_id={"dp": device}, device_id_type=MESH)
+    for j in range(1, n_z):
+        pl.semaphore_signal(
+            barrier, inc=1, device_id={"expert": lax.rem(z + j, n_z)}, device_id_type=MESH
+        )
+    pl.semaphore_wait(barrier, 3 + n_z - 1)
+
+    def to(device, src, dst, send, recv):
+        copy = pltpu.make_async_remote_copy(
+            src_ref=src,
+            dst_ref=dst,
+            send_sem=send,
+            recv_sem=recv,
+            device_id={"dp": device},
+            device_id_type=MESH,
+        )
+        copy.start()
+        return copy
+
+    sends = []
+    inputs = {}
+
+    def send_input(s):
+        inputs[s] = to(
+            peer, og_cols(owners[s] + flip), og_peer.at[s], in_send.at[s], in_recv.at[s]
+        )
+
+    send_input(DIAG)
+    loads[0].wait()
+    live = lax.broadcasted_iota(jnp.int32, hid_raw.shape, 0) < counts_ref[0]
+    hid_own[...] = jnp.where(live, hid_raw[...].astype(jnp.float32), 0.0).astype(jnp.bfloat16)
+    hid_copy = to(peer, hid_own, hid_peer, in_send.at[4], in_recv.at[4])
+    dense_a = to(
+        peer,
+        dpart_ref.at[pl.ds(pl.multiple_of((1 - core) * half, 8), half)],
+        d_one,
+        d_send.at[0],
+        d_recv.at[0],
+    )
+    for s in (XN, YN, OWN):
+        send_input(s)
+
+    def compute(s):
+        loads[1 + s].wait()
+        if s == DIAG:
+            hid_copy.wait_recv()
+        inputs[s].wait_recv()
+
+        @pl.loop(0, block // LANES)
+        def _(t):
+            at = pl.ds(pl.multiple_of(t * LANES, LANES), LANES)
+            dims = (((0,), (0,)), ((), ()))
+            part[s, at, :] = lax.dot_general(
+                og_own[s, :, at], hid_own[...], dims, preferred_element_type=jnp.float32
+            ) + lax.dot_general(
+                og_peer[s, :, at], hid_peer[...], dims, preferred_element_type=jnp.float32
+            )
+
+    def decoded(i):
+        scale = jnp.exp2(q_recv[i, pl.ds(block, 16), :].astype(jnp.int32)[0:1].astype(jnp.float32) * (1.0 / 256.0))
+        return q_recv[i, pl.ds(0, block), :].astype(jnp.int32).astype(jnp.float32) * scale
+
+    rs = {}
+
+    def send_sum(device, s, k, value=None):
+        i = s * chunks + k
+        if value is None:
+            value = part[s, :, cols(k)]
+        top = jnp.max(jnp.abs(value), axis=0, keepdims=True)
+        level = jnp.ceil(jnp.log2(jnp.maximum(top, 1e-30) * (1.0 / TOP)) * 256.0) + 1.0
+        q = jnp.round(value * jnp.exp2(level * (-1.0 / 256.0)))
+        q_send[i, pl.ds(0, block), :] = q.astype(jnp.int32).astype(jnp.int16)
+        q_send[i, pl.ds(block, 16), :] = (
+            jnp.broadcast_to(level, (16, LANES)).astype(jnp.int32).astype(jnp.int16)
+        )
+        rs[s, k] = to(device, q_send.at[i], q_recv.at[i], rs_send.at[i], rs_recv.at[i])
+
+    def first_hop(s, k):
+        send_sum((x_next, y_next)[k % 2] if s == DIAG else owners[s], s, k)
+
+    def second_hop(s, k):
+        rs[DIAG, k].wait_recv()
+        send_sum(owners[s], s, k, part[s, :, cols(k)] + decoded(DIAG * chunks + k))
+
+    compute(DIAG)
+    first_hop(DIAG, 0)
+    first_hop(DIAG, 1)
+    dense_a.wait_recv()
+    d_two[0] = dpart_ref[pl.ds(pl.multiple_of(core * half, 8), half), :] + d_one[...]
+    dense_b = to(x_next, d_two.at[0], d_two.at[1], d_send.at[1], d_recv.at[1])
+    compute(XN)
+    first_hop(XN, 0)
+    compute(YN)
+    first_hop(YN, 1)
+    for k in range(2, chunks):
+        first_hop(DIAG, k)
+    dense_b.wait_recv()
+    d_three[0] = d_two[0] + d_two[1]
+    dense_c = to(y_next, d_three.at[0], d_three.at[1], d_send.at[2], d_recv.at[2])
+    second_hop(XN, 1)
+    second_hop(YN, 0)
+    compute(OWN)
+    dense_c.wait_recv()
+    d_four[...] = d_three[0] + d_three[1]
+    dense_d = []
+    for j in range(1, n_z):
+        target = lax.rem(z + j, n_z)
+        source = lax.rem(z + n_z - j, n_z)
+        copy = pltpu.make_async_remote_copy(
+            src_ref=d_four,
+            dst_ref=d_z.at[j],
+            send_sem=d_send.at[3 + j],
+            recv_sem=d_recv.at[3 + j],
+            device_id={"expert": target},
+            device_id_type=MESH,
+        )
+        copy.start()
+        dense_d.append(copy)
+    for k in range(2, chunks):
+        first_hop((XN, YN)[k % 2], k)
+    for k in range(2, chunks):
+        second_hop((YN, XN)[k % 2], k)
+
+    ag = {}
+    stores = []
+    peers = []
+    for i in (5, 6, 7):
+        loads[i].wait()
+
+    def spread(s, k):
+        rows = pl.ds(pl.multiple_of(owners[s] * block, LANES), block)
+        i = s * chunks + k
+        src, dst = w_all.at[s, k], w_out.at[rows, cols(k)]
+        peers.append(to(peer, src, dst, peer_send.at[i], peer_recv.at[i]))
+        copy = pltpu.make_async_copy(src, dst, place_sem.at[i])
+        copy.start()
+        stores.append(copy)
+
+    def finish(k):
+        rs[XN, k].wait_recv()
+        rs[YN, k].wait_recv()
+        gradient = part[OWN, :, cols(k)] + decoded(XN * chunks + k) + decoded(YN * chunks + k)
+        master, moment, second = adamw_kernel(
+            gradient, p_s[:, cols(k)], m_s[:, cols(k)], v_s[:, cols(k)]
+        )
+        w_all[OWN, k] = master.astype(jnp.bfloat16)
+        for s, device in ((XN, x_next), (YN, y_next)):
+            ag[s, k] = to(
+                device,
+                w_all.at[OWN, k],
+                w_all.at[s, k],
+                ag_send.at[s * chunks + k],
+                ag_recv.at[s * chunks + k],
+            )
+        p_s[:, cols(k)] = master
+        m_s[:, cols(k)] = moment
+        v_s[:, cols(k)] = second
+        spread(OWN, k)
+        for i, (a, b) in enumerate(((p_s, p_out), (m_s, m_out), (v_s, v_out))):
+            copy = pltpu.make_async_copy(
+                a.at[:, cols(k)], b.at[:, cols(k)], store_sem.at[i * chunks + k]
+            )
+            copy.start()
+            stores.append(copy)
+
+    for k in range(chunks):
+        finish(k)
+
+    for copy in dense_d:
+        copy.wait_recv()
+    d_z[0] = d_four[...]
+    total = None
+    for zz in range(n_z):
+        term = d_z[lax.rem(z - zz + n_z, n_z)]
+        total = term if total is None else total + term
+    d_at = pl.ds(pl.multiple_of(core * half, 8), half)
+    d_tot[d_at, :] = total
+    dense_e = to(peer, d_tot.at[d_at], d_tot.at[d_at], d_send.at[3], d_recv.at[3])
+
+    for k in range(chunks):
+        s, device = ((XN, y_next), (YN, x_next))[k % 2]
+        ag[s, k].wait_recv()
+        ag[DIAG, k] = to(
+            device,
+            w_all.at[s, k],
+            w_all.at[DIAG, k],
+            ag_send.at[DIAG * chunks + k],
+            ag_recv.at[DIAG * chunks + k],
+        )
+        spread(s, k)
+        other = XN + YN - s
+        ag[other, k].wait_recv()
+        spread(other, k)
+
+    dense_e.wait_recv()
+    d_new = adamw_kernel(d_tot[...], dp_ref[...], dm_ref[...], dv_ref[...])
+    dp_out[...], dm_out[...], dv_out[...] = d_new
+
+    for k in range(chunks):
+        ag[DIAG, k].wait_recv()
+        spread(DIAG, k)
+
+    for copy in list(inputs.values()) + [hid_copy, dense_a, dense_b, dense_c, dense_e] + dense_d:
+        copy.wait_send()
+    for copy in list(rs.values()) + list(ag.values()):
+        copy.wait_send()
+    for copy in peers:
+        copy.wait()
+    for copy in stores:
+        copy.wait()
+
+
+def fused_on_device(
+    n_z,
+    hidden_act,
+    out_grad,
+    counts,
+    expert_master,
+    expert_mom,
+    expert_var,
+    dense_partial,
+    dense_master,
+    dense_mom,
+    dense_var,
+):
+    slots, width = hidden_act.shape
+    block = expert_master.shape[0]
+    chunks = width // LANES
+    gains = dense_master.shape[0]
+    rows = gains // LANES
+    half = rows // 2
+    f32, bf16, i16 = jnp.float32, jnp.bfloat16, jnp.int16
+    dma = pltpu.SemaphoreType.DMA
+    vmem = pl.BlockSpec(memory_space=pltpu.VMEM)
+    hbm = pl.BlockSpec(memory_space=pl.ANY)
+    outs = pl.pallas_call(
+        functools.partial(fused_kernel, n_z),
+        out_shape=[
+            jax.ShapeDtypeStruct((out_grad.shape[1], width), bf16),
+            *[jax.ShapeDtypeStruct((block, width), f32)] * 3,
+            *[jax.ShapeDtypeStruct((rows, LANES), f32)] * 3,
+        ],
+        in_specs=[pl.BlockSpec(memory_space=pltpu.SMEM)] + [hbm] * 5 + [vmem] * 4,
+        out_specs=[hbm] * 4 + [vmem] * 3,
+        scratch_shapes=[
+            pltpu.VMEM((slots, width), bf16),
+            pltpu.VMEM((slots, width), bf16),
+            pltpu.VMEM((slots, width), bf16),
+            pltpu.VMEM((4, slots, block), bf16),
+            pltpu.VMEM((4, slots, block), bf16),
+            pltpu.VMEM((4, block, width), f32),
+            pltpu.VMEM((3 * chunks, block + 16, LANES), i16),
+            pltpu.VMEM((3 * chunks, block + 16, LANES), i16),
+            pltpu.VMEM((block, width), f32),
+            pltpu.VMEM((block, width), f32),
+            pltpu.VMEM((block, width), f32),
+            pltpu.VMEM((4, chunks, block, LANES), bf16),
+            pltpu.VMEM((half, LANES), f32),
+            pltpu.VMEM((2, half, LANES), f32),
+            pltpu.VMEM((2, half, LANES), f32),
+            pltpu.VMEM((half, LANES), f32),
+            pltpu.VMEM((n_z, half, LANES), f32),
+            pltpu.VMEM((rows, LANES), f32),
+            dma((8,)),
+            dma((3 * chunks,)),
+            dma((5,)),
+            dma((5,)),
+            dma((3 * chunks,)),
+            dma((3 * chunks,)),
+            dma((3 * chunks,)),
+            dma((3 * chunks,)),
+            dma((4 * chunks,)),
+            dma((4 * chunks,)),
+            dma((4 * chunks,)),
+            dma((3 + n_z,)),
+            dma((3 + n_z,)),
+        ],
+        compiler_params=pltpu.CompilerParams(
+            collective_id=0, has_side_effects=True, vmem_limit_bytes=56 * 2**20
+        ),
+    )(
+        counts,
+        hidden_act,
+        out_grad,
+        expert_master,
+        expert_mom,
+        expert_var,
+        dense_partial.reshape(rows, LANES),
+        dense_master.reshape(rows, LANES),
+        dense_mom.reshape(rows, LANES),
+        dense_var.reshape(rows, LANES),
+    )
+    return tuple(outs[:4]) + tuple(a.reshape(gains) for a in outs[4:])
+
+
 def solution(mesh):
     in_specs = (
         P("dp", "expert"),
@@ -83,6 +482,9 @@
         P(),
         P(),
     )
+    body = on_device
+    if mesh.shape["dp"] == 8:
+        body = functools.partial(fused_on_device, mesh.shape["expert"])
     return jax.shard_map(
-        on_device, mesh=mesh, in_specs=in_specs, out_specs=out_specs, check_vma=False
-    )
+        body, mesh=mesh, in_specs=in_specs, out_specs=out_specs, check_vma=False
+    )

time: 201 us -> 93.4 us (0.46)
  waiting for transfers between devices: 99.5 us -> 0 us
  Pallas kernels: 0 us -> 77.7 us
  blocking collectives: 40.8 us -> 0 us
  between operations: 14.7 us -> 1.31 us
  matrix products: 12.6 us -> 0 us
  local copies, waits for them, and re-layouts: 25.2 us -> 14.2 us
  other arithmetic: 7.57 us -> 0 us
    reduce_scatter x1 -> x0, waiting for transfers between devices: 97.5 us -> none  [on_device(): lax.psum_scatter(lax.dot_general(out_grad, masked, (((0,), (0,)), ((), ()...]
    pallas_call x0 -> x1, Pallas kernels: none -> 77.7 us  [fused_on_device(): pl.pallas_call(functools.partial(fused_kernel, n_z), out_shape=[jax.Shape...]
    psum x1 -> x0, blocking collectives: 40.8 us -> none  [on_device(): dense_grad = lax.psum(dense_local, ('dp', 'expert'))]
    dot_general x1 -> x0, matrix products: 12.6 us -> none  [on_device(): lax.dot_general(out_grad, masked, (((0,), (0,)), ((), ())), preferred_ele...]
    unnamed x19, local copies, waits for them, and re-layouts: 25.2 us -> 14.2 us
    convert_element_type x1 -> x0, other arithmetic: 6.88 us -> none  [on_device(): master_new.astype(jnp.bfloat16)]
  transfers between devices with their start and end apart: 2 -> 0, of which waited for: 2 -> 0; matrix products, arithmetic and copies ran while one was open for 7% -> 0% of each run, Pallas kernels for 0% -> 0%
where the time goes in v1:
time: 93.4 us; the launch traced here: 93.2 us
  Pallas kernels  77.7 us (83%)
  local copies, waits for them, and re-layouts  14.2 us (15%)
  between operations  1.31 us (1%)
    pallas_call x1, Pallas kernels, fused_on_device(): pl.pallas_call(functools.partial(fused_kernel, n_z), out_shape=[jax.Shape...  77.7 us
    unnamed x19, local copies, waits for them, and re-layouts  14.2 us

profile of v1, /device:TPU:0, one launch (start us, length us, event | category | flops | bytes accessed | tf_op | source)
XLA Modules:
  0.0 93.2 jit_solution(5231657020104164208)
XLA Ops:
  1.3 77.7 %shard_map.153 = (bf16[7168,512]{1,0:T(8,128)(2,1)}, f32[896,512]{1,0:T(8,128)}, f32[896,512]{1,0:T(8,128)}, f32[896,512]{1,0:T(8,128)}, f32[112,128]{1,0:T(8,12...) custom-call(s32[1]{0:T(128)S(6)} %copy.24.counts_ref, bf16[512,512]{1,0:T(8,128)(2,1)} %hid_ref.1, bf16[512,7168]{1,0:T(8,128)(2,1)} %og_ref.1, ...), custom_call_target="tpu_custom_call" | custom-call | tf_op jit(solution)/shard_map/pallas_call | solution.py:403
  79.0 0.0 copy-start.2
  79.0 6.7 %copy.25 = bf16[7168,512]{1,0:T(8,128)(2,1)} copy(bf16[7168,512]{1,0:T(8,128)(2,1)} %get-tuple-element.28) | data formatting | bytes 14680064
  85.7 0.0 copy-done.2
  85.7 0.0 copy-start.1
  85.7 1.2 %copy.26 = f32[896,512]{1,0:T(8,128)} copy(f32[896,512]{1,0:T(8,128)S(1)} %copy-done.2) | data formatting | bytes 3670016
  87.0 0.9 copy-done.1
  87.9 0.0 copy-start
  87.9 1.2 %copy.27 = f32[896,512]{1,0:T(8,128)} copy(f32[896,512]{1,0:T(8,128)S(1)} %copy-done.1) | data formatting | bytes 3670016
  89.1 0.9 copy-done
  90.1 0.0 copy-start.5
  90.1 0.0 copy-start.4
  90.1 0.0 copy-start.3
  90.1 1.2 %copy.28 = f32[896,512]{1,0:T(8,128)} copy(f32[896,512]{1,0:T(8,128)S(1)} %copy-done) | data formatting | bytes 3670016
  91.3 0.0 copy-done.5
  91.3 0.6 copy.29
  91.9 0.0 copy-done.4
  91.9 0.6 copy.30
  92.6 0.0 copy-done.3
  92.6 0.6 copy.31
Async XLA Ops:
  79.0 6.7 %copy-start.2 = (f32[896,512]{1,0:T(8,128)S(1)}, f32[896,512]{1,0:T(8,128)}, u32[]{:S(2)}) copy-start(f32[896,512]{1,0:T(8,128)} %get-tuple-element.29) | copy-start | bytes 5505028
  85.7 2.2 %copy-start.1 = (f32[896,512]{1,0:T(8,128)S(1)}, f32[896,512]{1,0:T(8,128)}, u32[]{:S(2)}) copy-start(f32[896,512]{1,0:T(8,128)} %get-tuple-element.30) | copy-start | bytes 5505028
  87.9 2.2 %copy-start = (f32[896,512]{1,0:T(8,128)S(1)}, f32[896,512]{1,0:T(8,128)}, u32[]{:S(2)}) copy-start(f32[896,512]{1,0:T(8,128)} %get-tuple-element.31) | copy-start | bytes 5505028
  90.1 1.2 %copy-start.5 = (f32[112,128]{1,0:T(8,128)S(1)}, f32[112,128]{1,0:T(8,128)}, u32[]{:S(2)}) copy-start(f32[112,128]{1,0:T(8,128)} %get-tuple-element.18) | copy-start | bytes 172036
  90.1 1.9 %copy-start.4 = (f32[112,128]{1,0:T(8,128)S(1)}, f32[112,128]{1,0:T(8,128)}, u32[]{:S(2)}) copy-start(f32[112,128]{1,0:T(8,128)} %get-tuple-element.19) | copy-start | bytes 172036
  90.1 2.5 %copy-start.3 = (f32[112,128]{1,0:T(8,128)S(1)}, f32[112,128]{1,0:T(8,128)}, u32[]{:S(2)}) copy-start(f32[112,128]{1,0:T(8,128)} %get-tuple-element.20) | copy-start | bytes 172036

commit v2 on v1

--- a/solution.py
+++ b/solution.py
@@ -109,10 +109,6 @@
     part,
     q_send,
     q_recv,
-    p_s,
-    m_s,
-    v_s,
-    w_all,
     d_one,
     d_two,
     d_three,
@@ -120,7 +116,6 @@
     d_z,
     d_tot,
     load_sem,
-    store_sem,
     in_send,
     in_recv,
     rs_send,
@@ -129,7 +124,6 @@
     ag_recv,
     peer_send,
     peer_recv,
-    place_sem,
     d_send,
     d_recv,
 ):
@@ -158,7 +152,7 @@
     loads = [pltpu.make_async_copy(hid_ref, hid_raw, load_sem.at[0])]
     for s in range(4):
         loads.append(pltpu.make_async_copy(og_cols(owners[s]), og_own.at[s], load_sem.at[1 + s]))
-    for i, (a, b) in enumerate(((p_ref, p_s), (m_ref, m_s), (v_ref, v_s))):
+    for i, (a, b) in enumerate(((p_ref, p_out), (m_ref, m_out), (v_ref, v_out))):
         loads.append(pltpu.make_async_copy(a, b, load_sem.at[5 + i]))
     for copy in loads:
         copy.start()
@@ -289,46 +283,38 @@
         second_hop((YN, XN)[k % 2], k)
 
     ag = {}
-    stores = []
     peers = []
     for i in (5, 6, 7):
         loads[i].wait()
 
+    def at(s, k):
+        rows = pl.ds(pl.multiple_of(owners[s] * block, LANES), block)
+        return w_out.at[rows, cols(k)]
+
     def spread(s, k):
-        rows = pl.ds(pl.multiple_of(owners[s] * block, LANES), block)
         i = s * chunks + k
-        src, dst = w_all.at[s, k], w_out.at[rows, cols(k)]
-        peers.append(to(peer, src, dst, peer_send.at[i], peer_recv.at[i]))
-        copy = pltpu.make_async_copy(src, dst, place_sem.at[i])
-        copy.start()
-        stores.append(copy)
+        peers.append(to(peer, at(s, k), at(s, k), peer_send.at[i], peer_recv.at[i]))
 
     def finish(k):
         rs[XN, k].wait_recv()
         rs[YN, k].wait_recv()
         gradient = part[OWN, :, cols(k)] + decoded(XN * chunks + k) + decoded(YN * chunks + k)
         master, moment, second = adamw_kernel(
-            gradient, p_s[:, cols(k)], m_s[:, cols(k)], v_s[:, cols(k)]
-        )
-        w_all[OWN, k] = master.astype(jnp.bfloat16)
+            gradient, p_out[:, cols(k)], m_out[:, cols(k)], v_out[:, cols(k)]
+        )
+        at(OWN, k)[...] = master.astype(jnp.bfloat16)
         for s, device in ((XN, x_next), (YN, y_next)):
             ag[s, k] = to(
                 device,
-                w_all.at[OWN, k],
-                w_all.at[s, k],
+                at(OWN, k),
+                at(OWN, k),
                 ag_send.at[s * chunks + k],
                 ag_recv.at[s * chunks + k],
             )
-        p_s[:, cols(k)] = master
-        m_s[:, cols(k)] = moment
-        v_s[:, cols(k)] = second
+        p_out[:, cols(k)] = master
+        m_out[:, cols(k)] = moment
+        v_out[:, cols(k)] = second
         spread(OWN, k)
-        for i, (a, b) in enumerate(((p_s, p_out), (m_s, m_out), (v_s, v_out))):
-            copy = pltpu.make_async_copy(
-                a.at[:, cols(k)], b.at[:, cols(k)], store_sem.at[i * chunks + k]
-            )
-            copy.start()
-            stores.append(copy)
 
     for k in range(chunks):
         finish(k)
@@ -349,8 +335,8 @@
         ag[s, k].wait_recv()
         ag[DIAG, k] = to(
             device,
-            w_all.at[s, k],
-            w_all.at[DIAG, k],
+            at(s, k),
+            at(s, k),
             ag_send.at[DIAG * chunks + k],
             ag_recv.at[DIAG * chunks + k],
         )
@@ -373,7 +359,16 @@
         copy.wait_send()
     for copy in peers:
         copy.wait()
-    for copy in stores:
+
+
+def place_kernel(*refs):
+    count = len(refs) // 2
+    copies = [
+        pltpu.make_async_copy(refs[i], refs[count + i], refs[-1].at[i]) for i in range(count)
+    ]
+    for copy in copies:
+        copy.start()
+    for copy in copies:
         copy.wait()
 
 
@@ -403,12 +398,12 @@
     outs = pl.pallas_call(
         functools.partial(fused_kernel, n_z),
         out_shape=[
-            jax.ShapeDtypeStruct((out_grad.shape[1], width), bf16),
-            *[jax.ShapeDtypeStruct((block, width), f32)] * 3,
-            *[jax.ShapeDtypeStruct((rows, LANES), f32)] * 3,
+            pltpu.VMEM((out_grad.shape[1], width), bf16),
+            *[pltpu.VMEM((block, width), f32)] * 3,
+            *[pltpu.VMEM((rows, LANES), f32)] * 3,
         ],
         in_specs=[pl.BlockSpec(memory_space=pltpu.SMEM)] + [hbm] * 5 + [vmem] * 4,
-        out_specs=[hbm] * 4 + [vmem] * 3,
+        out_specs=[vmem] * 7,
         scratch_shapes=[
             pltpu.VMEM((slots, width), bf16),
             pltpu.VMEM((slots, width), bf16),
@@ -418,10 +413,6 @@
             pltpu.VMEM((4, block, width), f32),
             pltpu.VMEM((3 * chunks, block + 16, LANES), i16),
             pltpu.VMEM((3 * chunks, block + 16, LANES), i16),
-            pltpu.VMEM((block, width), f32),
-            pltpu.VMEM((block, width), f32),
-            pltpu.VMEM((block, width), f32),
-            pltpu.VMEM((4, chunks, block, LANES), bf16),
             pltpu.VMEM((half, LANES), f32),
             pltpu.VMEM((2, half, LANES), f32),
             pltpu.VMEM((2, half, LANES), f32),
@@ -429,7 +420,6 @@
             pltpu.VMEM((n_z, half, LANES), f32),
             pltpu.VMEM((rows, LANES), f32),
             dma((8,)),
-            dma((3 * chunks,)),
             dma((5,)),
             dma((5,)),
             dma((3 * chunks,)),
@@ -438,12 +428,11 @@
             dma((3 * chunks,)),
             dma((4 * chunks,)),
             dma((4 * chunks,)),
-            dma((4 * chunks,)),
             dma((3 + n_z,)),
             dma((3 + n_z,)),
         ],
         compiler_params=pltpu.CompilerParams(
-            collective_id=0, has_side_effects=True, vmem_limit_bytes=56 * 2**20
+            collective_id=0, has_side_effects=True, vmem_limit_bytes=44 * 2**20
         ),
     )(
         counts,
@@ -457,6 +446,14 @@
         dense_mom.reshape(rows, LANES),
         dense_var.reshape(rows, LANES),
     )
+    outs = pl.pallas_call(
+        place_kernel,
+        out_shape=[jax.ShapeDtypeStruct(a.shape, a.dtype) for a in outs],
+        in_specs=[hbm] * 7,
+        out_specs=[hbm] * 7,
+        scratch_shapes=[dma((7,))],
+        compiler_params=pltpu.CompilerParams(vmem_limit_bytes=2**20),
+    )(*outs)
     return tuple(outs[:4]) + tuple(a.reshape(gains) for a in outs[4:])
 
 

time: 93.4 us -> 82.9 us (0.89)
  local copies, waits for them, and re-layouts: 14.2 us -> 0 us
  Pallas kernels: 77.7 us -> 81.4 us
    unnamed x19 -> x0, local copies, waits for them, and re-layouts: 14.2 us -> none
    pallas_call x1 -> x2, Pallas kernels: 77.7 us -> 81.4 us  [the longest x1 76.6 us: fused_on_device(): pl.pallas_call(functools.partial(fused_kernel, n_z), out_shape=[pltpu.VME...]
where the time goes in v2:
time: 82.9 us; the launch traced here: 82.7 us
  Pallas kernels  81.4 us (98%)
  between operations  1.29 us (2%)
    pallas_call x1, Pallas kernels, fused_on_device(): pl.pallas_call(functools.partial(fused_kernel, n_z), out_shape=[pltpu.VME...  76.6 us
    pallas_call x1, Pallas kernels, fused_on_device(): pl.pallas_call(place_kernel, out_shape=[jax.ShapeDtypeStruct(a.shape, a.d...  4.82 us

profile of v2, /device:TPU:0, one launch (start us, length us, event | category | flops | bytes accessed | tf_op | source)
XLA Modules:
  0.0 82.7 jit_solution(3733027070902177700)
XLA Ops:
  1.3 76.6 %shard_map.153 = (bf16[7168,512]{1,0:T(8,128)(2,1)S(1)}, f32[896,512]{1,0:T(8,128)S(1)}, f32[896,512]{1,0:T(8,128)S(1)}, f32[896,512]{1,0:T(8,128)S(1)}, f32[112...) custom-call(s32[1]{0:T(128)S(6)} %copy.17.counts_ref, bf16[512,512]{1,0:T(8,128)(2,1)} %hid_ref.1, ...), custom_call_target="tpu_custom_call" | custom-call | tf_op jit(solution)/shard_map/pallas_call | solution.py:398
  77.9 4.8 %shard_map.154 = (bf16[7168,512]{1,0:T(8,128)(2,1)}, f32[896,512]{1,0:T(8,128)}, f32[896,512]{1,0:T(8,128)}, f32[896,512]{1,0:T(8,128)}, f32[112,128]{1,0:T(8,12...) custom-call(bf16[7168,512]{1,0:T(8,128)(2,1)S(1)} %get-tuple-element.21.refs_0_, f32[896,512]{1,0:T(8,128)S(1)} %get-tuple-element.22.refs_1_, ...), custom_call_target="tpu_custom_call" | custom-call | tf_op jit(solution)/shard_map/pallas_call | solution.py:449

commit v3 on v2

--- a/solution.py
+++ b/solution.py
@@ -90,10 +90,10 @@
     p_ref,
     m_ref,
     v_ref,
-    dpart_ref,
-    dp_ref,
-    dm_ref,
-    dv_ref,
+    dpart_hbm,
+    dp_hbm,
+    dm_hbm,
+    dv_hbm,
     w_out,
     p_out,
     m_out,
@@ -101,6 +101,10 @@
     dp_out,
     dm_out,
     dv_out,
+    dpart_ref,
+    dp_ref,
+    dm_ref,
+    dv_ref,
     hid_raw,
     hid_own,
     hid_peer,
@@ -154,6 +158,9 @@
         loads.append(pltpu.make_async_copy(og_cols(owners[s]), og_own.at[s], load_sem.at[1 + s]))
     for i, (a, b) in enumerate(((p_ref, p_out), (m_ref, m_out), (v_ref, v_out))):
         loads.append(pltpu.make_async_copy(a, b, load_sem.at[5 + i]))
+    gain_pairs = ((dpart_hbm, dpart_ref), (dp_hbm, dp_ref), (dm_hbm, dm_ref), (dv_hbm, dv_ref))
+    for i, (a, b) in enumerate(gain_pairs):
+        loads.append(pltpu.make_async_copy(a, b, load_sem.at[8 + i]))
     for copy in loads:
         copy.start()
 
@@ -191,6 +198,7 @@
     live = lax.broadcasted_iota(jnp.int32, hid_raw.shape, 0) < counts_ref[0]
     hid_own[...] = jnp.where(live, hid_raw[...].astype(jnp.float32), 0.0).astype(jnp.bfloat16)
     hid_copy = to(peer, hid_own, hid_peer, in_send.at[4], in_recv.at[4])
+    loads[8].wait()
     dense_a = to(
         peer,
         dpart_ref.at[pl.ds(pl.multiple_of((1 - core) * half, 8), half)],
@@ -201,20 +209,22 @@
     for s in (XN, YN, OWN):
         send_input(s)
 
-    def compute(s):
-        loads[1 + s].wait()
-        if s == DIAG:
-            hid_copy.wait_recv()
-        inputs[s].wait_recv()
+    def compute(s, lo=0, hi=None):
+        hi = width if hi is None else hi
+        if lo == 0:
+            loads[1 + s].wait()
+            if s == DIAG:
+                hid_copy.wait_recv()
+            inputs[s].wait_recv()
 
         @pl.loop(0, block // LANES)
         def _(t):
             at = pl.ds(pl.multiple_of(t * LANES, LANES), LANES)
             dims = (((0,), (0,)), ((), ()))
-            part[s, at, :] = lax.dot_general(
-                og_own[s, :, at], hid_own[...], dims, preferred_element_type=jnp.float32
+            part[s, at, lo:hi] = lax.dot_general(
+                og_own[s, :, at], hid_own[:, lo:hi], dims, preferred_element_type=jnp.float32
             ) + lax.dot_general(
-                og_peer[s, :, at], hid_peer[...], dims, preferred_element_type=jnp.float32
+                og_peer[s, :, at], hid_peer[:, lo:hi], dims, preferred_element_type=jnp.float32
             )
 
     def decoded(i):
@@ -243,7 +253,8 @@
         rs[DIAG, k].wait_recv()
         send_sum(owners[s], s, k, part[s, :, cols(k)] + decoded(DIAG * chunks + k))
 
-    compute(DIAG)
+    split = width // 2
+    compute(DIAG, 0, split)
     first_hop(DIAG, 0)
     first_hop(DIAG, 1)
     dense_a.wait_recv()
@@ -253,6 +264,7 @@
     first_hop(XN, 0)
     compute(YN)
     first_hop(YN, 1)
+    compute(DIAG, split)
     for k in range(2, chunks):
         first_hop(DIAG, k)
     dense_b.wait_recv()
@@ -346,6 +358,8 @@
         spread(other, k)
 
     dense_e.wait_recv()
+    for i in (9, 10, 11):
+        loads[i].wait()
     d_new = adamw_kernel(d_tot[...], dp_ref[...], dm_ref[...], dv_ref[...])
     dp_out[...], dm_out[...], dv_out[...] = d_new
 
@@ -402,9 +416,10 @@
             *[pltpu.VMEM((block, width), f32)] * 3,
             *[pltpu.VMEM((rows, LANES), f32)] * 3,
         ],
-        in_specs=[pl.BlockSpec(memory_space=pltpu.SMEM)] + [hbm] * 5 + [vmem] * 4,
+        in_specs=[pl.BlockSpec(memory_space=pltpu.SMEM)] + [hbm] * 9,
         out_specs=[vmem] * 7,
         scratch_shapes=[
+            *[pltpu.VMEM((rows, LANES), f32)] * 4,
             pltpu.VMEM((slots, width), bf16),
             pltpu.VMEM((slots, width), bf16),
             pltpu.VMEM((slots, width), bf16),
@@ -419,7 +434,7 @@
             pltpu.VMEM((half, LANES), f32),
             pltpu.VMEM((n_z, half, LANES), f32),
             pltpu.VMEM((rows, LANES), f32),
-            dma((8,)),
+            dma((12,)),
             dma((5,)),
             dma((5,)),
             dma((3 * chunks,)),

time: 82.9 us -> 81.6 us (0.984)
  Pallas kernels: 81.4 us -> 80.2 us
    pallas_call x1, Pallas kernels: 76.6 us -> 75.4 us  [fused_on_device(): pl.pallas_call(functools.partial(fused_kernel, n_z), out_shape=[pltpu.VME...]
where the time goes in v3:
time: 81.6 us; the launch traced here: 81.5 us
  Pallas kernels  80.2 us (98%)
  between operations  1.29 us (2%)
    pallas_call x1, Pallas kernels, fused_on_device(): pl.pallas_call(functools.partial(fused_kernel, n_z), out_shape=[pltpu.VME...  75.4 us
    pallas_call x1, Pallas kernels, fused_on_device(): pl.pallas_call(place_kernel, out_shape=[jax.ShapeDtypeStruct(a.shape, a.d...  4.82 us

profile of v3, /device:TPU:0, one launch (start us, length us, event | category | flops | bytes accessed | tf_op | source)
XLA Modules:
  0.0 81.5 jit_solution(1090986435222269311)
XLA Ops:
  1.3 75.4 %shard_map.153 = (bf16[7168,512]{1,0:T(8,128)(2,1)S(1)}, f32[896,512]{1,0:T(8,128)S(1)}, f32[896,512]{1,0:T(8,128)S(1)}, f32[896,512]{1,0:T(8,128)S(1)}, f32[112...) custom-call(s32[1]{0:T(128)S(6)} %copy.17.counts_ref, bf16[512,512]{1,0:T(8,128)(2,1)} %hid_ref.1, ...), custom_call_target="tpu_custom_call" | custom-call | tf_op jit(solution)/shard_map/pallas_call | solution.py:412
  76.7 4.8 %shard_map.154 = (bf16[7168,512]{1,0:T(8,128)(2,1)}, f32[896,512]{1,0:T(8,128)}, f32[896,512]{1,0:T(8,128)}, f32[896,512]{1,0:T(8,128)}, f32[112,128]{1,0:T(8,12...) custom-call(bf16[7168,512]{1,0:T(8,128)(2,1)S(1)} %get-tuple-element.21.refs_0_, f32[896,512]{1,0:T(8,128)S(1)} %get-tuple-element.22.refs_1_, ...), custom_call_target="tpu_custom_call" | custom-call | tf_op jit(solution)/shard_map/pallas_call | solution.py:464
